TPU v7x, 8 devices: a whole 2x2x1 slice. The times are simulated.
8 devices in a mesh: fsdp: 8 (over z, y, x, core).
Axes of the slice: x: 2, y: 2, z: 1, core: 2. Of those that a mesh axis runs over, the one named last changes fastest.
Arguments:
- x: bfloat16 [2, 16384, 2048], P(None, 'fsdp')
- g: bfloat16 [2, 16384, 2048], P(None, 'fsdp')
- w1: bfloat16 [1, 2048, 8192], P(None, 'fsdp')
- w2: bfloat16 [1, 8192, 2048], P(None, 'fsdp')
Outputs:
- output 1: bfloat16 [2, 16384, 2048], P(None, 'fsdp')
- output 2: float32 [1, 2048, 8192], P(None, 'fsdp')
- output 3: float32 [1, 8192, 2048], P(None, 'fsdp')
All inputs are finite; a program needn't handle non-finite values.
Results may differ from a plain program's by a relative error of at most 0.001.
Values are sent between devices in bfloat16 or wider.
A program may use at most 1 GiB of HBM per device.

v0:
```python
import jax
import jax.numpy as jnp
from jax import lax
from jax.sharding import PartitionSpec as P

AX = "fsdp"


def _gelu_bwd(a, e):
    return jax.vjp(jax.nn.gelu, a)[1](e)[0]


def solution(mesh):
    spec = P(None, AX, None)

    def body(x, g, w1, w2):
        layers = w1.shape[0]

        def micro(acc, xg):
            cur, gy = xg
            saved = []
            for l in range(layers):
                v1 = lax.all_gather(w1[l], AX, axis=0, tiled=True)
                v2 = lax.all_gather(w2[l], AX, axis=0, tiled=True)
                a = jnp.dot(cur, v1, preferred_element_type=jnp.float32).astype(jnp.bfloat16)
                h = jax.nn.gelu(a.astype(jnp.float32)).astype(jnp.bfloat16)
                saved.append((cur, a))
                cur = (cur.astype(jnp.float32) + jnp.dot(h, v2, preferred_element_type=jnp.float32)).astype(jnp.bfloat16)
            d1, d2 = [None] * layers, [None] * layers
            for l in reversed(range(layers)):
                xl, a = saved[l]
                v2 = lax.all_gather(w2[l], AX, axis=0, tiled=True)
                h = jax.nn.gelu(a.astype(jnp.float32)).astype(jnp.bfloat16)
                e = jnp.dot(gy, v2.T, preferred_element_type=jnp.float32)
                da = _gelu_bwd(a.astype(jnp.float32), e).astype(jnp.bfloat16)
                p2 = jnp.dot(h.T, gy, preferred_element_type=jnp.float32)
                p1 = jnp.dot(xl.T, da, preferred_element_type=jnp.float32)
                d2[l] = acc[1][l] + lax.psum_scatter(p2, AX, scatter_dimension=0, tiled=True)
                d1[l] = acc[0][l] + lax.psum_scatter(p1, AX, scatter_dimension=0, tiled=True)
                if l > 0:
                    v1 = lax.all_gather(w1[l], AX, axis=0, tiled=True)
                    gy = (gy.astype(jnp.float32) + jnp.dot(da, v1.T, preferred_element_type=jnp.float32)).astype(jnp.bfloat16)
            return (jnp.stack(d1), jnp.stack(d2)), cur

        zeros = (jnp.zeros(w1.shape, jnp.float32), jnp.zeros(w2.shape, jnp.float32))
        (d1, d2), y = lax.scan(micro, zeros, (x, g))
        return y, d1, d2

    return jax.shard_map(body, mesh=mesh, in_specs=(spec, spec, spec, spec),
                         out_specs=(spec, spec, spec), check_vma=False)
```

profile of v0, /device:TPU:1, one launch (start us, length us, event | category | flops | bytes accessed | tf_op | source)
XLA Modules:
  0.0 2210.3 jit_solution(5530449541326431317)
XLA Ops:
  7.2 4.5 broadcast_in_dim.17
  11.6 4.4 broadcast_in_dim.16
  16.0 2187.2 %while.16 = (s32[]{:T(128)}, f32[1,256,8192]{2,1,0:T(8,128)}, f32[1,1024,2048]{2,1,0:T(8,128)}, bf16[2,2048,2048]{2,1,0:T(8,128)(2,1)}, bf16[2,2048,2048]{2,1,0:...) while((s32[]{:T(128)}, f32[1,256,8192]{2,1,0:T(8,128)}, ...), condition=%wide.region_3.4_spmd, body=%wide.region_0.3_spmd.sunk | while | flops 344318803968 | bytes 1216348416 | solution.py:46
  16.0 0.7 all-gather.9.cloned.1.call-update
  16.8 0.7 all-gather.11.cloned.1.call-update
  17.5 0.0 reduce-scatter.5.cloned.1.call-start
  17.5 158.6 %all-gather.9.cloned.1.call-done = bf16[1,2048,8192]{2,1,0:T(8,128)(2,1)} async-done(((bf16[1,256,8192]{2,1,0:T(8,128)(2,1)}), bf16[1,2048,8192]{2,1,0:T(8,128)(2,1)}) %all-gather.9.cloned.1.call-update) | async-done | bytes 33554448 | tf_op jit(solution)/shard_map/while/body/eval_jaxpr/all_gather | solution.py:23
  176.1 77.9 %fusion.109 = bf16[2048,8192]{1,0:T(8,128)(2,1)} fusion(bf16[1,2048,8192]{2,1,0:T(8,128)(2,1)} %all-gather.9.cloned.1.call-done, bf16[2,2048,2048]{2,1,0:T(8,128)(2,1)} %get-tuple-element.196, s32[]{:T(128)S(6)} %copy.12), kind=kOutput, calls=%fused_computation.22.clone.2 | convolution fusion | flops 68736253952 | bytes 75497472 | tf_op jit(solution)/shard_map/while/body/eval_jaxpr/dot_general | solution.py:25
  254.0 93.0 %fusion.113 = f32[8192,2048]{1,0:T(8,128)} fusion(bf16[2,2048,2048]{2,1,0:T(8,128)(2,1)} %get-tuple-element.197, s32[]{:T(128)S(6)} %copy.12, bf16[2048,8192]{1,0:T(8,128)(2,1)} %fusion.109), kind=kOutput, calls=%fused_computation.28.clone.3 | convolution fusion | flops 68887248896 | bytes 109051904 | tf_op jit(solution)/shard_map/while/body/eval_jaxpr/dot_general | solution.py:36
  347.0 0.0 reduce-scatter.3.cloned.1.call-start
  347.1 121.3 %fusion.110 = bf16[2048,8192]{1,0:T(8,128)(2,1)} fusion(bf16[2048,8192]{1,0:T(8,128)(2,1)} %fusion.109, bf16[1,8192,2048]{2,1,0:T(8,128)(2,1)} %all-gather.11.cloned.1.call-done, bf16[2,2048,2048]{2,1,0:T(8,128)(2,1)} %get-tuple-element.197, s32[]{:T(128)S(6)} %copy.12), kind=kOutput, calls=%fused_computation.8.clone.clone.2.clone.1 | convolution fusion | flops 69071798272 | bytes 109051904 | tf_op jit(solution)/shard_map/while/body/eval_jaxpr/dot_general | solution.py:34
  468.3 79.7 %fusion.111 = f32[2048,8192]{1,0:T(8,128)} fusion(s32[]{:T(128)S(6)} %copy.12, bf16[2,2048,2048]{2,1,0:T(8,128)(2,1)} %get-tuple-element.196, bf16[2048,8192]{1,0:T(8,128)(2,1)} %fusion.110), kind=kOutput, calls=%fused_computation.21.clone.3 | convolution fusion | flops 68719476736 | bytes 109051904 | tf_op jit(solution)/shard_map/while/body/eval_jaxpr/dot_general | solution.py:37
  548.0 91.8 %fusion.115 = bf16[2,2048,2048]{2,1,0:T(8,128)(2,1)} fusion(bf16[2,2048,2048]{2,1,0:T(8,128)(2,1)} %get-tuple-element.186, s32[]{:T(128)S(6)} %copy.12, bf16[1,8192,2048]{2,1,0:T(8,128)(2,1)} %all-gather.11.cloned.1.call-done, bf16[2,2048,2048]{2,1,0:T(8,128)(2,1)} %get-tuple-element.196, bf16[2048,8192]{1,0:T(8,128)(2,1)} %fusion.109), kind=kOutput, calls=%fused_computation.25.clone.2 | convolution fusion | flops 68899831808 | bytes 83886080 | tf_op jit(solution)/shard_map/while/body/eval_jaxpr/dot_general | solution.py:28
  639.8 81.4 %reduce-scatter.5.cloned.1.call-done = f32[1024,2048]{1,0:T(8,128)} async-done(((f32[8192,2048]{1,0:T(8,128)}), f32[1024,2048]{1,0:T(8,128)}) %reduce-scatter.5.cloned.1.call-update) | async-done | bytes 8388624 | tf_op jit(solution)/shard_map/while/body/eval_jaxpr/reduce_scatter | solution.py:38
  721.2 11.9 fusion.114
  733.0 366.3 %reduce-scatter.3.cloned.1.call-done = f32[256,8192]{1,0:T(8,128)} async-done(((f32[2048,8192]{1,0:T(8,128)}), f32[256,8192]{1,0:T(8,128)}) %reduce-scatter.3.cloned.1.call-update) | async-done | bytes 8388624 | tf_op jit(solution)/shard_map/while/body/eval_jaxpr/reduce_scatter | solution.py:39
  1099.3 10.4 fusion.112
  1110.0 0.0 all-gather.9.cloned.1.call-start
  1110.0 0.5 all-gather.9.cloned.1.call-update
  1110.6 0.5 all-gather.11.cloned.1.call-update
  1111.1 0.0 reduce-scatter.5.cloned.1.call-start
  1111.2 157.0 %all-gather.9.cloned.1.call-done = bf16[1,2048,8192]{2,1,0:T(8,128)(2,1)} async-done(((bf16[1,256,8192]{2,1,0:T(8,128)(2,1)}), bf16[1,2048,8192]{2,1,0:T(8,128)(2,1)}) %all-gather.9.cloned.1.call-update) | async-done | bytes 33554448 | tf_op jit(solution)/shard_map/while/body/eval_jaxpr/all_gather | solution.py:23
  1268.2 77.9 %fusion.109 = bf16[2048,8192]{1,0:T(8,128)(2,1)} fusion(bf16[1,2048,8192]{2,1,0:T(8,128)(2,1)} %all-gather.9.cloned.1.call-done, bf16[2,2048,2048]{2,1,0:T(8,128)(2,1)} %get-tuple-element.196, s32[]{:T(128)S(6)} %copy.12), kind=kOutput, calls=%fused_computation.22.clone.2 | convolution fusion | flops 68736253952 | bytes 75497472 | tf_op jit(solution)/shard_map/while/body/eval_jaxpr/dot_general | solution.py:25
  1346.1 93.2 %fusion.113 = f32[8192,2048]{1,0:T(8,128)} fusion(bf16[2,2048,2048]{2,1,0:T(8,128)(2,1)} %get-tuple-element.197, s32[]{:T(128)S(6)} %copy.12, bf16[2048,8192]{1,0:T(8,128)(2,1)} %fusion.109), kind=kOutput, calls=%fused_computation.28.clone.3 | convolution fusion | flops 68887248896 | bytes 109051904 | tf_op jit(solution)/shard_map/while/body/eval_jaxpr/dot_general | solution.py:36
  1439.3 0.0 reduce-scatter.3.cloned.1.call-start
  1439.4 121.0 %fusion.110 = bf16[2048,8192]{1,0:T(8,128)(2,1)} fusion(bf16[2048,8192]{1,0:T(8,128)(2,1)} %fusion.109, bf16[1,8192,2048]{2,1,0:T(8,128)(2,1)} %all-gather.11.cloned.1.call-done, bf16[2,2048,2048]{2,1,0:T(8,128)(2,1)} %get-tuple-element.197, s32[]{:T(128)S(6)} %copy.12), kind=kOutput, calls=%fused_computation.8.clone.clone.2.clone.1 | convolution fusion | flops 69071798272 | bytes 109051904 | tf_op jit(solution)/shard_map/while/body/eval_jaxpr/dot_general | solution.py:34
  1560.4 79.7 %fusion.111 = f32[2048,8192]{1,0:T(8,128)} fusion(s32[]{:T(128)S(6)} %copy.12, bf16[2,2048,2048]{2,1,0:T(8,128)(2,1)} %get-tuple-element.196, bf16[2048,8192]{1,0:T(8,128)(2,1)} %fusion.110), kind=kOutput, calls=%fused_computation.21.clone.3 | convolution fusion | flops 68719476736 | bytes 109051904 | tf_op jit(solution)/shard_map/while/body/eval_jaxpr/dot_general | solution.py:37
  1640.2 92.0 %fusion.115 = bf16[2,2048,2048]{2,1,0:T(8,128)(2,1)} fusion(bf16[2,2048,2048]{2,1,0:T(8,128)(2,1)} %get-tuple-element.186, s32[]{:T(128)S(6)} %copy.12, bf16[1,8192,2048]{2,1,0:T(8,128)(2,1)} %all-gather.11.cloned.1.call-done, bf16[2,2048,2048]{2,1,0:T(8,128)(2,1)} %get-tuple-element.196, bf16[2048,8192]{1,0:T(8,128)(2,1)} %fusion.109), kind=kOutput, calls=%fused_computation.25.clone.2 | convolution fusion | flops 68899831808 | bytes 83886080 | tf_op jit(solution)/shard_map/while/body/eval_jaxpr/dot_general | solution.py:28
  1732.1 81.4 %reduce-scatter.5.cloned.1.call-done = f32[1024,2048]{1,0:T(8,128)} async-done(((f32[8192,2048]{1,0:T(8,128)}), f32[1024,2048]{1,0:T(8,128)}) %reduce-scatter.5.cloned.1.call-update) | async-done | bytes 8388624 | tf_op jit(solution)/shard_map/while/body/eval_jaxpr/reduce_scatter | solution.py:38
  1813.5 11.9 fusion.114
  1825.4 366.4 %reduce-scatter.3.cloned.1.call-done = f32[256,8192]{1,0:T(8,128)} async-done(((f32[2048,8192]{1,0:T(8,128)}), f32[256,8192]{1,0:T(8,128)}) %reduce-scatter.3.cloned.1.call-update) | async-done | bytes 8388624 | tf_op jit(solution)/shard_map/while/body/eval_jaxpr/reduce_scatter | solution.py:39
  2191.8 10.4 fusion.112
  (10 shorter events, 0.2 us)
Async XLA Ops:
  16.0 160.1 %all-gather.9.cloned.1.call-start = ((), (), s32[]{:S(2)}) async-start(), calls=%async_computation.2 | async-start | bytes 37748736 | tf_op jit(solution)/shard_map/while/body/eval_jaxpr/all_gather | solution.py:23
  16.7 330.3 %all-gather.11.cloned.1.call-start = ((), (), s32[]{:S(2)}) async-start(), calls=%async_computation.3 | async-start | bytes 37748736 | tf_op jit(solution)/shard_map/while/body/eval_jaxpr/all_gather | solution.py:32
  17.5 703.7 %reduce-scatter.5.cloned.1.call-start = ((), (), s32[]{:S(2)}) async-start(), calls=%async_computation.5 | async-start | bytes 75497472 | tf_op jit(solution)/shard_map/while/body/eval_jaxpr/reduce_scatter | solution.py:38
  347.0 752.3 %reduce-scatter.3.cloned.1.call-start = ((), (), s32[]{:S(2)}) async-start(), calls=%async_computation.4 | async-start | bytes 75497472 | tf_op jit(solution)/shard_map/while/body/eval_jaxpr/reduce_scatter | solution.py:39
  1110.0 158.2 %all-gather.9.cloned.1.call-start = ((), (), s32[]{:S(2)}) async-start(), calls=%async_computation.2 | async-start | bytes 37748736 | tf_op jit(solution)/shard_map/while/body/eval_jaxpr/all_gather | solution.py:23
  1110.5 328.9 %all-gather.11.cloned.1.call-start = ((), (), s32[]{:S(2)}) async-start(), calls=%async_computation.3 | async-start | bytes 37748736 | tf_op jit(solution)/shard_map/while/body/eval_jaxpr/all_gather | solution.py:32
  1111.1 702.4 %reduce-scatter.5.cloned.1.call-start = ((), (), s32[]{:S(2)}) async-start(), calls=%async_computation.5 | async-start | bytes 75497472 | tf_op jit(solution)/shard_map/while/body/eval_jaxpr/reduce_scatter | solution.py:38
  1439.3 752.4 %reduce-scatter.3.cloned.1.call-start = ((), (), s32[]{:S(2)}) async-start(), calls=%async_computation.4 | async-start | bytes 75497472 | tf_op jit(solution)/shard_map/while/body/eval_jaxpr/reduce_scatter | solution.py:39
Sparse Core Ops, SparseCore 0:
  18.6 157.4 all-gather.8
  177.9 155.1 all-gather.10
  347.1 374.0 reduce-scatter.4
  724.5 374.7 reduce-scatter.2
  1112.3 155.8 all-gather.8
  1269.9 155.1 all-gather.10
  1439.4 374.0 reduce-scatter.4
  1817.0 374.7 reduce-scatter.2
where the time goes:
time: 2210 us
  waiting for transfers between devices  1210 us (55%)
  matrix products  927 us (42%)
  other arithmetic  44.6 us (2%)
    reduce_scatter x2, waiting for transfers between devices, micro(): lax.psum_scatter(p1, AX, scatter_dimension=0, tiled=True)  733 us
    all_gather x2, waiting for transfers between devices, micro(): v1 = lax.all_gather(w1[l], AX, axis=0, tiled=True)  316 us
    dot_general x2, matrix products, micro(): e = jnp.dot(gy, v2.T, preferred_element_type=jnp.float32)  242 us
    dot_general x2, matrix products, micro(): p2 = jnp.dot(h.T, gy, preferred_element_type=jnp.float32)  186 us
    dot_general x2, matrix products, micro(): jnp.dot(h, v2, preferred_element_type=jnp.float32)  184 us
    reduce_scatter x2, waiting for transfers between devices, micro(): lax.psum_scatter(p2, AX, scatter_dimension=0, tiled=True)  163 us
    dot_general x2, matrix products, micro(): p1 = jnp.dot(xl.T, da, preferred_element_type=jnp.float32)  159 us
    dot_general x2, matrix products, micro(): jnp.dot(cur, v1, preferred_element_type=jnp.float32).astype(jnp.bfloat16)  156 us
  transfers between devices with their start and end apart: 8, of which 6 were waited for; matrix products, arithmetic and copies ran while one was open for 43% of the time, Pallas kernels for 0%

commit v1 on v0

v1 whole, which is shorter than its diff:
```python
import functools

import jax
import jax.numpy as jnp
from jax import lax
from jax.experimental import pallas as pl
from jax.experimental.pallas import tpu as pltpu
from jax.sharding import PartitionSpec as P

AX = "fsdp"
F32 = jnp.float32
BF16 = jnp.bfloat16
MESH = pl.DeviceIdType.MESH
C0 = 0.7978845608028654
C1 = 0.044715
D = 2048
HF = 4096
TOK = 4096
T = 2 * TOK
B = 1024
SUB = 256
VMEM = 60 * 2**20


def _gelu(a):
    return a * (0.5 * (1.0 + jnp.tanh(C0 * (a + C1 * (a * a * a)))))


def _gelu_grad(a):
    a2 = a * a
    t = jnp.tanh(C0 * (a + C1 * (a2 * a)))
    return 0.5 * (1.0 + t) + (0.5 * a) * (1.0 - t * t) * (C0 + (3.0 * C1 * C0) * a2)


def _kernel(x, g, w1, w2,
            y, dw2, o1, o1r, r1f, xa, ga, w1g, w2g, aa, ha, da, s2, r2, s1, r1, yp, yr,
            xs, xr, w1s, w1r, w2s, w2r, s2s, s2r, s1s, s1r, os, orr, ys, yrs):
    me = lax.axis_index(AX)
    c, q = me % 2, me // 2
    qx, qy = q % 2, q // 2
    nx, ny, nd = 2 * qy + (1 - qx), 2 * (1 - qy) + qx, 3 - q
    dev = lambda chip, core: 2 * chip + core
    peer = dev(q, 1 - c)

    def blk(i):
        return 2 * ((qy + i // 2) % 2) + (qx + i % 2) % 2

    def rdma(src, dst, ss, rs, to):
        return pltpu.make_async_remote_copy(src_ref=src, dst_ref=dst, send_sem=ss, recv_sem=rs,
                                            device_id=(to,), device_id_type=MESH)

    cx = rdma(x, xa.at[pl.ds(TOK, TOK)], xs.at[0], xr.at[0], peer)
    cg = rdma(g, ga.at[pl.ds(TOK, TOK)], xs.at[1], xr.at[1], peer)

    def w1_rows(owner, j):
        return w1g.at[pl.ds(owner * 256, 256), pl.ds(j * B, B)]

    def w1_out(j):
        def one(role, rsem, p, to):
            return rdma(w1.at[:, pl.ds((2 * j + p) * B, B)], w1_rows(me, j), w1s.at[j, role], w1r.at[j, rsem], to)
        return [one(1, 1 + c, 0, dev(nx, 0)), one(2, 1 + c, 1, dev(nx, 1)),
                one(3, 3 + c, 0, dev(ny, 0)), one(4, 3 + c, 1, dev(ny, 1)),
                one(0, 0, 1 - c, peer)]

    def w1_in(j):
        def one(owner, rsem):
            return rdma(w1_rows(owner, j), w1_rows(owner, j), w1s.at[j, 0], w1r.at[j, rsem], peer)
        return [one(peer, 0), one(dev(nx, 0), 1), one(dev(nx, 1), 2), one(dev(ny, 0), 3), one(dev(ny, 1), 4)]

    def w1_relay(j):
        ra, rb = w1_rows(dev(nx, 0), j), w1_rows(dev(ny, 1), j)
        return [rdma(ra, ra, w1s.at[j, 5], w1r.at[j, 5], dev(ny, c)),
                rdma(rb, rb, w1s.at[j, 6], w1r.at[j, 6], dev(nx, c))]

    def w1_relay_in(j):
        ra, rb = w1_rows(dev(nd, 0), j), w1_rows(dev(nd, 1), j)
        return [rdma(ra, ra, w1s.at[j, 5], w1r.at[j, 5], peer), rdma(rb, rb, w1s.at[j, 6], w1r.at[j, 6], peer)]

    def w2_rows(chip, lo, n):
        return w2g.at[pl.ds(chip * B + lo, n)]

    w2_out = [rdma(w2, w2_rows(q, 0, B), w2s.at[0], w2r.at[0], dev(nx, c)),
              rdma(w2, w2_rows(q, 0, B), w2s.at[1], w2r.at[1], dev(ny, c))]
    w2_in = [rdma(w2_rows(nx, 0, B), w2_rows(nx, 0, B), w2s.at[0], w2r.at[0], peer),
             rdma(w2_rows(ny, 0, B), w2_rows(ny, 0, B), w2s.at[1], w2r.at[1], peer)]
    w2_relay = [rdma(w2_rows(nx, 0, B // 2), w2_rows(nx, 0, B // 2), w2s.at[2], w2r.at[2], dev(ny, c)),
                rdma(w2_rows(ny, B // 2, B // 2), w2_rows(ny, B // 2, B // 2), w2s.at[3], w2r.at[3], dev(nx, c))]
    w2_relay_in = [rdma(w2_rows(nd, 0, B // 2), w2_rows(nd, 0, B // 2), w2s.at[2], w2r.at[2], peer),
                   rdma(w2_rows(nd, B // 2, B // 2), w2_rows(nd, B // 2, B // 2), w2s.at[3], w2r.at[3], peer)]

    p2 = [rdma(s2.at[k], r2.at[k], s2s.at[k], s2r.at[k], dev(nx if k in (0, 2, 4) else ny, c)) for k in range(6)]
    p1d = [rdma(s1.at[k], r1.at[k], s1s.at[k, 0], s1r.at[k, 0], dev(nx if k == 0 else ny, c)) for k in range(2)]
    p1 = [[rdma(s1.at[k, pl.ds(256 * p, 256)], r1f.at[k - 2, c], s1s.at[k, p], s1r.at[k, c], dev(nx if k in (2, 4) else ny, p))
           for p in range(2)] for k in range(2, 6)]
    p1_in = [[rdma(s1.at[k, pl.ds(256 * p, 256)], r1f.at[k - 2, p], s1s.at[k, p], s1r.at[k, p], peer)
              for p in range(2)] for k in range(2, 6)]
    co = rdma(o1.at[:, pl.ds(256 * (1 - c), 256)], o1r, os.at[0], orr.at[0], peer)
    cy = rdma(yp, yr, ys.at[0], yrs.at[0], peer)

    def copy_body(*refs):
        n = len(refs) // 2
        for i in range(n):
            refs[n + i][...] = refs[i][...]

    def a_phase(j):
        def body(x_ref, w_ref, a_ref, h_ref):
            @pl.when((pl.program_id(0) == 6) & (j < 3))
            def _():
                for d in w1_in(j + 1):
                    d.wait_recv()
                for d in w1_relay(j + 1):
                    d.start()

            @pl.when((pl.program_id(0) == 6) & (j < 2))
            def _():
                for d in w1_out(j + 2):
                    d.start()

            @pl.when((pl.program_id(0) == 6) & (j == 2))
            def _():
                for d in w2_out:
                    d.start()

            for n in range(B // SUB):
                s = slice(n * SUB, (n + 1) * SUB)
                a = jnp.dot(x_ref[...], w_ref[:, s], preferred_element_type=F32).astype(BF16)
                a_ref[:, s] = a
                h_ref[:, s] = _gelu(a.astype(F32)).astype(BF16)

        out = pl.BlockSpec((B, B), lambda i: (i, j))
        pltpu.emit_pipeline(body, grid=(T // B,),
                            in_specs=[pl.BlockSpec((B, D), lambda i: (i, 0)), pl.BlockSpec((D, B), lambda i: (0, j))],
                            out_specs=[out, out])(xa, w1g, aa, ha)

    def e_phase(lo, n):
        def body(g_ref, w_ref, a_ref, d_ref):
            for m in range(B // SUB):
                s = slice(m * SUB, (m + 1) * SUB)
                e = lax.dot_general(g_ref[...], w_ref[s, :], (((1,), (1,)), ((), ())), preferred_element_type=F32)
                d_ref[:, s] = (_gelu_grad(a_ref[:, s].astype(F32)) * e).astype(BF16)

        act = pl.BlockSpec((B, B), lambda i, k: (k, blk(i + lo)))
        pltpu.emit_pipeline(body, grid=(n, T // B),
                            in_specs=[pl.BlockSpec((B, D), lambda i, k: (k, 0)),
                                      pl.BlockSpec((B, D), lambda i, k: (blk(i + lo), 0)), act],
                            out_specs=[act])(ga, w2g, aa, da)

    def tn(lhs, rhs, out, m, n, li, ri, out_spec, recv=()):
        def body(l_ref, r_ref, *rest):
            o_ref = rest[-1]
            @pl.when(pl.program_id(1) == 0)
            def _():
                init = jnp.zeros(o_ref.shape, F32)
                for r in rest[:-1]:
                    init = init + r[...].reshape(o_ref.shape)
                o_ref[...] = init
            o_ref[...] += lax.dot_general(l_ref[...], r_ref[...], (((0,), (0,)), ((), ())),
                                          preferred_element_type=F32).reshape(o_ref.shape)

        pltpu.emit_pipeline(body, grid=(2, T // B),
                            in_specs=[pl.BlockSpec((B, m), lambda i, k: (k, li(i))), pl.BlockSpec((B, n), lambda i, k: (k, ri(i)))]
                            + [pl.BlockSpec((1, m, n), functools.partial(lambda f, i, k: (f(i), 0, 0), f)) for _, f in recv],
                            out_specs=[out_spec])(lhs, rhs, *[r for r, _ in recv], out)

    half = pl.BlockSpec((1, B, B), lambda i, k: (i, 0, 0))
    half1 = pl.BlockSpec((1, 512, D), lambda i, k: (i, 0, 0))
    near = lambda i: (1 - i) * nx + i * ny
    d2 = lambda slot, li, ri, recv=(): tn(ha, ga, s2.at[pl.ds(slot, 2)], B, B, li, ri, half, recv)
    d1 = lambda slot, li, ri, recv=(): tn(xa, da, s1.at[pl.ds(slot, 2)], 512, D, li, ri, half1, recv)

    def y_phase(own):
        def body(h_ref, w_ref, *rest):
            v = jnp.dot(h_ref[...], w_ref[...], preferred_element_type=F32)
            if own:
                x_ref, r_ref, o_ref = rest
                o_ref[...] = (x_ref[...].astype(F32) + (v + r_ref[...])).astype(BF16)
            else:
                rest[0][...] = v

        bm = 512
        base = 0 if own else TOK // bm
        col = pl.BlockSpec((bm, B), lambda n, i: (i, n))
        pltpu.emit_pipeline(body, grid=(2, TOK // bm),
                            in_specs=[pl.BlockSpec((bm, HF), lambda n, i: (i + base, 0)), pl.BlockSpec((HF, B), lambda n, i: (0, n))]
                            + ([col, col] if own else []),
                            out_specs=[col])(ha, w2g, *([x, yr] if own else []), y if own else yp)

    barrier = pltpu.get_barrier_semaphore()
    friends = [peer, dev(nx, 0), dev(nx, 1), dev(ny, 0), dev(ny, 1)]
    for d in friends:
        pl.semaphore_signal(barrier, inc=1, device_id=(d,), device_id_type=MESH)
    pl.semaphore_wait(barrier, len(friends))

    for d in w1_out(0):
        d.start()
    cx.start()
    cg.start()
    pltpu.emit_pipeline(copy_body, grid=(4,), in_specs=[pl.BlockSpec((256, B), lambda i: (0, 2 * i + c))],
                        out_specs=[pl.BlockSpec((256, B), lambda i: (me, i))])(w1, w1g)
    for d in w1_in(0):
        d.wait_recv()
    for d in w1_relay(0):
        d.start()
    for d in w1_out(1):
        d.start()
    row = pl.BlockSpec((B, D), lambda i: (i, 0))
    pltpu.emit_pipeline(copy_body, grid=(TOK // B,), in_specs=[row, row], out_specs=[row, row])(
        x, g, xa.at[pl.ds(0, TOK)], ga.at[pl.ds(0, TOK)])
    pltpu.emit_pipeline(copy_body, grid=(2,), in_specs=[pl.BlockSpec((B // 2, D), lambda i: (i, 0))],
                        out_specs=[pl.BlockSpec((B // 2, D), lambda i: (2 * q + i, 0))])(w2, w2g)
    cx.wait_recv()

    @pl.loop(0, 4)
    def _(j):
        for d in w1_relay_in(j):
            d.wait_recv()
        a_phase(j)

    cg.wait_recv()
    d2(0, lambda i: nd, lambda i: i)
    p2[0].start()
    p2[1].start()
    for d in w2_in:
        d.wait_recv()
    for d in w2_relay:
        d.start()
    d2(2, near, lambda i: i)
    p2[2].start()
    p2[3].start()
    e_phase(0, 3)
    for d in w2_relay_in:
        d.wait_recv()
    e_phase(3, 1)
    d1(0, lambda i: nd, lambda i: i)
    p1d[0].start()
    p1d[1].start()
    p2[0].wait_recv()
    p2[1].wait_recv()
    d2(4, near, lambda i: 1 - i, [(r2, lambda i: 1 - i)])
    p2[4].start()
    p2[5].start()
    d1(2, near, lambda i: i)
    for k in (0, 1):
        for d in p1[k]:
            d.start()
    y_phase(False)
    cy.start()
    p1d[0].wait_recv()
    p1d[1].wait_recv()
    d1(4, near, lambda i: 1 - i, [(r1, lambda i: 1 - i)])
    for k in (2, 3):
        for d in p1[k]:
            d.start()
    tn(xa, da, o1, 512, D, lambda i: q, lambda i: i, half1)
    co.start()
    for k in range(2, 6):
        p2[k].wait_recv()
    tn(ha, ga, dw2, B, B, lambda i: q, lambda i: i, pl.BlockSpec((B, B), lambda i, k: (0, i)),
       [(r2, lambda i: 2 + i), (r2, lambda i: 5 - i)])
    cy.wait_recv()
    y_phase(True)
    co.wait_recv()
    for pair in p1_in:
        for d in pair:
            d.wait_recv()
    for d in [cx, cg, co, cy] + w2_out + w2_relay + p2 + p1d + [d for pair in p1 for d in pair]:
        d.wait_send()

    @pl.loop(0, 4)
    def _(j):
        for d in w1_out(j) + w1_relay(j):
            d.wait_send()


def solution(mesh):
    spec = P(None, AX, None)

    def body(x, g, w1, w2):
        c = lax.axis_index(AX) % 2
        shape = lambda s, t: jax.ShapeDtypeStruct(s, t)
        dma = lambda *s: pltpu.SemaphoreType.DMA(s)
        hbm = pl.BlockSpec(memory_space=pl.ANY)
        outs = [
            shape((TOK, D), BF16), shape((B, D), F32), shape((2, 512, D), F32), shape((2, 256, D), F32), shape((4, 2, 256, D), F32),
            shape((T, D), BF16), shape((T, D), BF16), shape((D, HF), BF16), shape((HF, D), BF16),
            shape((T, HF), BF16), shape((T, HF), BF16), shape((T, HF), BF16),
            shape((6, B, B), F32), shape((6, B, B), F32), shape((6, 512, D), F32), shape((2, 512, D), F32),
            shape((TOK, D), F32), shape((TOK, D), F32),
        ]
        res = pl.pallas_call(
            _kernel,
            out_shape=outs,
            in_specs=[hbm] * 4,
            out_specs=[hbm] * len(outs),
            scratch_shapes=[dma(2), dma(2), dma(4, 7), dma(4, 7), dma(4), dma(4), dma(6), dma(6), dma(6, 2), dma(6, 2),
                            dma(1), dma(1), dma(1), dma(1)],
            compiler_params=pltpu.CompilerParams(collective_id=0, has_side_effects=True, vmem_limit_bytes=VMEM),
            name="step",
        )(x.reshape(TOK, D), g.reshape(TOK, D), w1[0], w2[0])
        y, dw2, o1, o1r, r1f = res[:5]
        mine = lax.dynamic_slice_in_dim(o1, 256 * c, 256, 1)
        own = jnp.where(c == 0, jnp.stack([mine, o1r]), jnp.stack([o1r, mine]))
        far = jnp.stack([r1f[0] + r1f[3], r1f[1] + r1f[2]], axis=1)
        dw1 = (own + far).reshape(2, 2, 256, 2, B).transpose(2, 1, 3, 0, 4).reshape(1, 256, 8192)
        return y.reshape(2, TOK // 2, D), dw1, dw2[None]

    return jax.shard_map(body, mesh=mesh, in_specs=(spec, spec, spec, spec),
                         out_specs=(spec, spec, spec), check_vma=False)
```

time: 2210 us -> 1100 us (0.50)
  waiting for transfers between devices: 1210 us -> 0 us
  Pallas kernels: 0 us -> 998 us
  matrix products: 927 us -> 0 us
  local copies, waits for them, and re-layouts: 8.83 us -> 72.7 us
    pallas_call x0 -> x1, Pallas kernels: none -> 998 us  [body(): pl.pallas_call(_kernel, out_shape=outs, in_specs=[hbm] * 4, out_specs=[hb...]
    dot_general x10 -> x0, matrix products: 927 us -> none  [the longest x2 242 us: micro(): e = jnp.dot(gy, v2.T, preferred_element_type=jnp.float32)]
    reduce_scatter x4 -> x0, waiting for transfers between devices: 895 us -> none  [the longest x2 733 us: micro(): lax.psum_scatter(p1, AX, scatter_dimension=0, tiled=True)]
    all_gather x4 -> x0, waiting for transfers between devices: 316 us -> none  [the longest x2 316 us: micro(): v1 = lax.all_gather(w1[l], AX, axis=0, tiled=True)]
    another operation x4 -> x0, other arithmetic: 44.6 us -> none  [micro(): return ((jnp.stack(d1), jnp.stack(d2)), cur)]
  transfers between devices with their start and end apart: 8 -> 0, of which waited for: 6 -> 0; matrix products, arithmetic and copies ran while one was open for 43% -> 0% of each run, Pallas kernels for 0% -> 0%
where the time goes in v1:
time: 1100 us
  Pallas kernels  998 us (91%)
  local copies, waits for them, and re-layouts  72.7 us (7%)
  other arithmetic  25.1 us (2%)
    pallas_call x1, Pallas kernels, body(): pl.pallas_call(_kernel, out_shape=outs, in_specs=[hbm] * 4, out_specs=[hb...  998 us
    unnamed x2, local copies, waits for them, and re-layouts  22 us

profile of v1, /device:TPU:1, one launch (start us, length us, event | category | flops | bytes accessed | tf_op | source)
XLA Modules:
  0.0 1096.8 jit_solution(16801341825502275493)
XLA Ops:
  0.6 997.9 %step.1 = (bf16[4096,2048]{1,0:T(8,128)(2,1)}, f32[1024,2048]{1,0:T(8,128)}, f32[2,512,2048]{2,1,0:T(8,128)}, f32[2,256,2048]{2,1,0:T(8,128)}, f32[4,2,256,2048]...) custom-call(bf16[4096,2048]{1,0:T(8,128)(2,1)} %bitcast.13, ...), custom_call_target="tpu_custom_call" | custom-call | tf_op jit(solution)/shard_map/step/pallas_call | solution.py:290
  998.6 6.6 stack.20
  1005.1 4.7 constant_dynamic-slice_fusion
  1009.8 6.6 stack.19
  1016.4 11.9 %slice_add_fusion.1 = (f32[1,2,256,2048]{3,2,1,0:T(8,128)}, f32[1,2,256,2048]{3,2,1,0:T(8,128)}) fusion(f32[4,2,256,2048]{3,2,1,0:T(8,128)} %get-tuple-element.11), kind=kLoop, calls=%fused_computation.4 | loop fusion | flops 2097152 | bytes 25165824 | tf_op jit(solution)/shard_map/add | solution.py:303
  1028.3 6.6 add.44
  1034.8 6.6 add.42
  1041.4 13.3 %fusion.1 = f32[256,2,2,2,1024]{4,2,0,3,1:T(2,128)S(1)} fusion(f32[1,2,256,2,1024]{4,3,2,0,1:T(2,128)} %bitcast.16, f32[1,2,256,2,1024]{4,3,2,0,1:T(2,128)} %stack.19, f32[2,1,256,2,1024]{4,3,2,0,1:T(2,128)} %add.44, f32[2,1,256,2,1024]{4,3,2,0,1:T(2,128)} %add.42, pred[]{:T(512)S(6)} %eq.5), kind=kLoop, calls=%fused_computation.2 | loop fusion | flops 10485760 | bytes 25165824 | tf_op jit(solution)/shard_map/transpose | solution.py:304
  1054.7 7.9 copy.9
  1062.6 11.8 %reshape.72 = f32[1,256,8192]{2,1,0:T(8,128)} reshape(f32[256,2,2,2,1024]{4,3,2,1,0:T(2,128)} %copy.9) | data formatting | bytes 16777216 | tf_op jit(solution)/shard_map/reshape | solution.py:304
  1074.4 14.2 %copy.12 = bf16[2,2048,2048]{2,1,0:T(8,128)(2,1)} copy(bf16[2,2048,2048]{2,1,0:T(8,128)(2,1)} %bitcast.15) | data formatting | bytes 33554432
  1088.5 7.9 copy.13

commit v2 on v1

--- a/solution.py
+++ b/solution.py
@@ -23,13 +23,15 @@
 
 
 def _gelu(a):
-    return a * (0.5 * (1.0 + jnp.tanh(C0 * (a + C1 * (a * a * a)))))
+    t = jnp.tanh(a * (C0 + (C0 * C1) * (a * a)))
+    b = 0.5 * a
+    return b + b * t
 
 
 def _gelu_grad(a):
     a2 = a * a
-    t = jnp.tanh(C0 * (a + C1 * (a2 * a)))
-    return 0.5 * (1.0 + t) + (0.5 * a) * (1.0 - t * t) * (C0 + (3.0 * C1 * C0) * a2)
+    t = jnp.tanh(a * (C0 + (C0 * C1) * a2))
+    return (0.5 + 0.5 * t) + ((1.0 - t * t) * a) * (0.5 * C0 + (1.5 * C0 * C1) * a2)
 
 
 def _kernel(x, g, w1, w2,
@@ -123,9 +125,9 @@
 
             for n in range(B // SUB):
                 s = slice(n * SUB, (n + 1) * SUB)
-                a = jnp.dot(x_ref[...], w_ref[:, s], preferred_element_type=F32).astype(BF16)
-                a_ref[:, s] = a
-                h_ref[:, s] = _gelu(a.astype(F32)).astype(BF16)
+                a = jnp.dot(x_ref[s, :], w_ref[...], preferred_element_type=F32).astype(BF16)
+                a_ref[s, :] = a
+                h_ref[s, :] = _gelu(a.astype(F32)).astype(BF16)
 
         out = pl.BlockSpec((B, B), lambda i: (i, j))
         pltpu.emit_pipeline(body, grid=(T // B,),
@@ -136,8 +138,8 @@
         def body(g_ref, w_ref, a_ref, d_ref):
             for m in range(B // SUB):
                 s = slice(m * SUB, (m + 1) * SUB)
-                e = lax.dot_general(g_ref[...], w_ref[s, :], (((1,), (1,)), ((), ())), preferred_element_type=F32)
-                d_ref[:, s] = (_gelu_grad(a_ref[:, s].astype(F32)) * e).astype(BF16)
+                e = lax.dot_general(g_ref[s, :], w_ref[...], (((1,), (1,)), ((), ())), preferred_element_type=F32)
+                d_ref[s, :] = (_gelu_grad(a_ref[s, :].astype(F32)) * e).astype(BF16)
 
         act = pl.BlockSpec((B, B), lambda i, k: (k, blk(i + lo)))
         pltpu.emit_pipeline(body, grid=(n, T // B),
@@ -154,8 +156,10 @@
                 for r in rest[:-1]:
                     init = init + r[...].reshape(o_ref.shape)
                 o_ref[...] = init
-            o_ref[...] += lax.dot_general(l_ref[...], r_ref[...], (((0,), (0,)), ((), ())),
-                                          preferred_element_type=F32).reshape(o_ref.shape)
+            for i in range(m // SUB):
+                s = slice(i * SUB, (i + 1) * SUB)
+                o_ref[..., s, :] += lax.dot_general(l_ref[:, s], r_ref[...], (((0,), (0,)), ((), ())),
+                                                    preferred_element_type=F32).reshape(o_ref.shape[:-2] + (SUB, n))
 
         pltpu.emit_pipeline(body, grid=(2, T // B),
                             in_specs=[pl.BlockSpec((B, m), lambda i, k: (k, li(i))), pl.BlockSpec((B, n), lambda i, k: (k, ri(i)))]
@@ -214,51 +218,64 @@
     def _(j):
         for d in w1_relay_in(j):
             d.wait_recv()
-        a_phase(j)
+        with jax.named_scope("pa"):
+            a_phase(j)
 
     cg.wait_recv()
-    d2(0, lambda i: nd, lambda i: i)
+    with jax.named_scope("d2diag"):
+        d2(0, lambda i: nd, lambda i: i)
     p2[0].start()
     p2[1].start()
     for d in w2_in:
         d.wait_recv()
     for d in w2_relay:
         d.start()
-    d2(2, near, lambda i: i)
+    with jax.named_scope("d2raw"):
+        d2(2, near, lambda i: i)
     p2[2].start()
     p2[3].start()
-    e_phase(0, 3)
+    with jax.named_scope("e3"):
+        e_phase(0, 3)
     for d in w2_relay_in:
         d.wait_recv()
-    e_phase(3, 1)
-    d1(0, lambda i: nd, lambda i: i)
+    with jax.named_scope("e1"):
+        e_phase(3, 1)
+    with jax.named_scope("d1diag"):
+        d1(0, lambda i: nd, lambda i: i)
     p1d[0].start()
     p1d[1].start()
     p2[0].wait_recv()
     p2[1].wait_recv()
-    d2(4, near, lambda i: 1 - i, [(r2, lambda i: 1 - i)])
+    with jax.named_scope("d2add"):
+        d2(4, near, lambda i: 1 - i, [(r2, lambda i: 1 - i)])
     p2[4].start()
     p2[5].start()
-    d1(2, near, lambda i: i)
+    with jax.named_scope("d1raw"):
+        d1(2, near, lambda i: i)
     for k in (0, 1):
         for d in p1[k]:
             d.start()
-    y_phase(False)
+    with jax.named_scope("ypeer"):
+        y_phase(False)
     cy.start()
     p1d[0].wait_recv()
     p1d[1].wait_recv()
-    d1(4, near, lambda i: 1 - i, [(r1, lambda i: 1 - i)])
+    with jax.named_scope("d1add"):
+        d1(4, near, lambda i: 1 - i, [(r1, lambda i: 1 - i)])
     for k in (2, 3):
         for d in p1[k]:
             d.start()
-    tn(xa, da, o1, 512, D, lambda i: q, lambda i: i, half1)
+    with jax.named_scope("d1own"):
+        tn(xa, da, o1, 512, D, lambda i: q, lambda i: i, half1)
     co.start()
     for k in range(2, 6):
         p2[k].wait_recv()
-    tn(ha, ga, dw2, B, B, lambda i: q, lambda i: i, pl.BlockSpec((B, B), lambda i, k: (0, i)),
-       [(r2, lambda i: 2 + i), (r2, lambda i: 5 - i)])
+    with jax.named_scope("d2own"):
+        tn(ha, ga, dw2, B, B, lambda i: q, lambda i: i, pl.BlockSpec((B, B), lambda i, k: (0, i)),
+           [(r2, lambda i: 2 + i), (r2, lambda i: 5 - i)])
     cy.wait_recv()
-    y_phase(True)
+    with jax.named_scope("yown"):
+        y_phase(True)
     co.wait_recv()
     for pair in p1_in:
         for d in pair:
@@ -270,6 +287,13 @@
     def _(j):
         for d in w1_out(j) + w1_relay(j):
             d.wait_send()
+
+
+def _finish(c_ref, y, dw2, o1, o1r, fa, fb, y_out, dw1_out, dw2_out):
+    y_out[...] = y[...]
+    dw2_out[...] = dw2[...]
+    own = jnp.where(pl.program_id(0) < 8, o1[0], o1r[0])
+    dw1_out[...] = own + (fa[0, 0] + fb[0, 0])
 
 
 def solution(mesh):
@@ -298,11 +322,31 @@
             name="step",
         )(x.reshape(TOK, D), g.reshape(TOK, D), w1[0], w2[0])
         y, dw2, o1, o1r, r1f = res[:5]
-        mine = lax.dynamic_slice_in_dim(o1, 256 * c, 256, 1)
-        own = jnp.where(c == 0, jnp.stack([mine, o1r]), jnp.stack([o1r, mine]))
-        far = jnp.stack([r1f[0] + r1f[3], r1f[1] + r1f[2]], axis=1)
-        dw1 = (own + far).reshape(2, 2, 256, 2, B).transpose(2, 1, 3, 0, 4).reshape(1, 256, 8192)
-        return y.reshape(2, TOK // 2, D), dw1, dw2[None]
+        part = lambda s, c: (s // 8) * (1 - c[0]) + (1 - s // 8) * c[0]
+        n, t, r = (lambda s: (s // 4) % 2), (lambda s: (s // 2) % 2), (lambda s: s % 2)
+        mine = lambda s: jnp.minimum(s, 7)
+        other = lambda s: jnp.maximum(s, 8)
+        y_spec = pl.BlockSpec((TOK // 16, D), lambda s, c: (s, 0))
+        dw2_spec = pl.BlockSpec((B // 16, D), lambda s, c: (s, 0))
+        y, dw1, dw2 = pl.pallas_call(
+            _finish,
+            grid_spec=pltpu.PrefetchScalarGridSpec(
+                num_scalar_prefetch=1,
+                grid=(16,),
+                in_specs=[
+                    y_spec, dw2_spec,
+                    pl.BlockSpec((1, 128, B), lambda s, c: (n(mine(s)), 2 * c[0] + r(mine(s)), t(mine(s)))),
+                    pl.BlockSpec((1, 128, B), lambda s, c: (n(other(s)), r(other(s)), t(other(s)))),
+                    pl.BlockSpec((1, 1, 128, B), lambda s, c: (n(s), part(s, c), r(s), t(s))),
+                    pl.BlockSpec((1, 1, 128, B), lambda s, c: (3 - n(s), part(s, c), r(s), t(s))),
+                ],
+                out_specs=[y_spec, pl.BlockSpec((128, B), lambda s, c: (r(s), 2 * (2 * n(s) + t(s)) + part(s, c))), dw2_spec],
+            ),
+            out_shape=[shape((TOK, D), BF16), shape((256, 8192), F32), shape((B, D), F32)],
+            compiler_params=pltpu.CompilerParams(dimension_semantics=("arbitrary",)),
+            name="finish",
+        )(c[None], y, dw2, o1, o1r, r1f, r1f)
+        return y.reshape(2, TOK // 2, D), dw1[None], dw2[None]
 
     return jax.shard_map(body, mesh=mesh, in_specs=(spec, spec, spec, spec),
                          out_specs=(spec, spec, spec), check_vma=False)

time: 1100 us -> 991 us (0.901)
  local copies, waits for them, and re-layouts: 72.7 us -> 0 us
  other arithmetic: 25.1 us -> 0 us
    pallas_call x1, Pallas kernels: 998 us -> 960 us  [body(): pl.pallas_call(_kernel, out_shape=outs, in_specs=[hbm] * 4, out_specs=[hb...]
    pallas_call x0 -> x1, Pallas kernels: none -> 30.1 us  [body(): pl.pallas_call(_finish, grid_spec=pltpu.PrefetchScalarGridSpec(num_scalar...]
    unnamed x2 -> x0, local copies, waits for them, and re-layouts: 22 us -> none
    transpose x1 -> x0, other arithmetic: 13.3 us -> none  [body(): (own + far).reshape(2, 2, 256, 2, B).transpose(2, 1, 3, 0, 4)]
    add x2 -> x0, local copies, waits for them, and re-layouts: 13.2 us -> none  [body(): far = jnp.stack([r1f[0] + r1f[3], r1f[1] + r1f[2]], axis=1)]
    another operation x2 -> x0, local copies, waits for them, and re-layouts: 13.1 us -> none  [body(): own = jnp.where(c == 0, jnp.stack([mine, o1r]), jnp.stack([o1r, mine]))]
    add x1 -> x0, other arithmetic: 11.9 us -> none  [body(): far = jnp.stack([r1f[0] + r1f[3], r1f[1] + r1f[2]], axis=1)]
    reshape x1 -> x0, local copies, waits for them, and re-layouts: 11.8 us -> none  [body(): (own + far).reshape(2, 2, 256, 2, B).transpose(2, 1, 3, 0, 4)]
where the time goes in v2:
time: 991 us
  Pallas kernels  990 us (100%)
    pallas_call x1, Pallas kernels, body(): pl.pallas_call(_kernel, out_shape=outs, in_specs=[hbm] * 4, out_specs=[hb...  960 us
    pallas_call x1, Pallas kernels, body(): pl.pallas_call(_finish, grid_spec=pltpu.PrefetchScalarGridSpec(num_scalar...  30.1 us

profile of v2, /device:TPU:1, one launch (start us, length us, event | category | flops | bytes accessed | tf_op | source)
XLA Modules:
  0.0 990.7 jit_solution(1718318261272958327)
XLA Ops:
  0.6 959.9 %step.1 = (bf16[4096,2048]{1,0:T(8,128)(2,1)}, f32[1024,2048]{1,0:T(8,128)}, f32[2,512,2048]{2,1,0:T(8,128)}, f32[2,256,2048]{2,1,0:T(8,128)}, f32[4,2,256,2048]...) custom-call(bf16[4096,2048]{1,0:T(8,128)(2,1)} %bitcast.8, ...), custom_call_target="tpu_custom_call" | custom-call | tf_op jit(solution)/shard_map/step/pallas_call | solution.py:314
  960.5 30.1 %finish.1 = (bf16[4096,2048]{1,0:T(8,128)(2,1)}, f32[256,8192]{1,0:T(8,128)}, f32[1024,2048]{1,0:T(8,128)}) custom-call(s32[1]{0:T(128)} %bitcast.c_ref, bf16[4096,2048]{1,0:T(8,128)(2,1)} %get-tuple-element.11.y, f32[1024,2048]{1,0:T(8,128)} %get-tuple-element.12.dw2, f32[2,512,2048]{2,1,0:T(8,128)} %get-tuple-element.13.o1, ...), custom_call_target="tpu_custom_call" | custom-call | tf_op jit(solution)/shard_map/finish/pallas_call | solution.py:331

commit v3 on v2

v3 whole, which is shorter than its diff:
```python
import functools

import jax
import jax.numpy as jnp
from jax import lax
from jax.experimental import pallas as pl
from jax.experimental.pallas import tpu as pltpu
from jax.sharding import PartitionSpec as P

AX = "fsdp"
F32 = jnp.float32
BF16 = jnp.bfloat16
MESH = pl.DeviceIdType.MESH
C0 = 0.7978845608028654
C1 = 0.044715
D = 2048
HF = 4096
TOK = 4096
T = 2 * TOK
B = 1024
SUB = 256
VMEM = 60 * 2**20


def _gelu(a):
    t = jnp.tanh(a * (C0 + (C0 * C1) * (a * a)))
    b = 0.5 * a
    return b + b * t


def _gelu_grad(a):
    a2 = a * a
    t = jnp.tanh(a * (C0 + (C0 * C1) * a2))
    return (0.5 + 0.5 * t) + ((1.0 - t * t) * a) * (0.5 * C0 + (1.5 * C0 * C1) * a2)


def _kernel(x, g, w1, w2,
            ha, w2g, yr, y0, dw2, s1, o1r, r1f, xa, ga, w1g, aa, da, s2, r2, r1, yp,
            xs, xr, w1s, w1r, w2s, w2r, s2s, s2r, s1s, s1r, os, orr, ys, yrs):
    me = lax.axis_index(AX)
    c, q = me % 2, me // 2
    qx, qy = q % 2, q // 2
    nx, ny, nd = 2 * qy + (1 - qx), 2 * (1 - qy) + qx, 3 - q
    dev = lambda chip, core: 2 * chip + core
    peer = dev(q, 1 - c)

    def blk(i):
        return 2 * ((qy + i // 2) % 2) + (qx + i % 2) % 2

    def rdma(src, dst, ss, rs, to):
        return pltpu.make_async_remote_copy(src_ref=src, dst_ref=dst, send_sem=ss, recv_sem=rs,
                                            device_id=(to,), device_id_type=MESH)

    cx = rdma(x, xa.at[pl.ds(TOK, TOK)], xs.at[0], xr.at[0], peer)
    cg = rdma(g, ga.at[pl.ds(TOK, TOK)], xs.at[1], xr.at[1], peer)

    def w1_rows(owner, j):
        return w1g.at[pl.ds(owner * 256, 256), pl.ds(j * B, B)]

    def w1_out(j):
        def one(role, rsem, p, to):
            return rdma(w1.at[:, pl.ds((2 * j + p) * B, B)], w1_rows(me, j), w1s.at[j, role], w1r.at[j, rsem], to)
        return [one(1, 1 + c, 0, dev(nx, 0)), one(2, 1 + c, 1, dev(nx, 1)),
                one(3, 3 + c, 0, dev(ny, 0)), one(4, 3 + c, 1, dev(ny, 1)),
                one(0, 0, 1 - c, peer)]

    def w1_in(j):
        def one(owner, rsem):
            return rdma(w1_rows(owner, j), w1_rows(owner, j), w1s.at[j, 0], w1r.at[j, rsem], peer)
        return [one(peer, 0), one(dev(nx, 0), 1), one(dev(nx, 1), 2), one(dev(ny, 0), 3), one(dev(ny, 1), 4)]

    def w1_relay(j):
        ra, rb = w1_rows(dev(nx, 0), j), w1_rows(dev(ny, 1), j)
        return [rdma(ra, ra, w1s.at[j, 5], w1r.at[j, 5], dev(ny, c)),
                rdma(rb, rb, w1s.at[j, 6], w1r.at[j, 6], dev(nx, c))]

    def w1_relay_in(j):
        ra, rb = w1_rows(dev(nd, 0), j), w1_rows(dev(nd, 1), j)
        return [rdma(ra, ra, w1s.at[j, 5], w1r.at[j, 5], peer), rdma(rb, rb, w1s.at[j, 6], w1r.at[j, 6], peer)]

    def w2_rows(chip, lo, n):
        return w2g.at[pl.ds(chip * B + lo, n)]

    w2_out = [rdma(w2, w2_rows(q, 0, B), w2s.at[0], w2r.at[0], dev(nx, c)),
              rdma(w2, w2_rows(q, 0, B), w2s.at[1], w2r.at[1], dev(ny, c))]
    w2_in = [rdma(w2_rows(nx, 0, B), w2_rows(nx, 0, B), w2s.at[0], w2r.at[0], peer),
             rdma(w2_rows(ny, 0, B), w2_rows(ny, 0, B), w2s.at[1], w2r.at[1], peer)]
    w2_relay = [rdma(w2_rows(nx, 0, B // 2), w2_rows(nx, 0, B // 2), w2s.at[2], w2r.at[2], dev(ny, c)),
                rdma(w2_rows(ny, B // 2, B // 2), w2_rows(ny, B // 2, B // 2), w2s.at[3], w2r.at[3], dev(nx, c))]
    w2_relay_in = [rdma(w2_rows(nd, 0, B // 2), w2_rows(nd, 0, B // 2), w2s.at[2], w2r.at[2], peer),
                   rdma(w2_rows(nd, B // 2, B // 2), w2_rows(nd, B // 2, B // 2), w2s.at[3], w2r.at[3], peer)]

    p2 = [rdma(s2.at[k], r2.at[k], s2s.at[k], s2r.at[k], dev(nx if k in (0, 2, 4) else ny, c)) for k in range(6)]
    p1d = [rdma(s1.at[k], r1.at[k], s1s.at[k, 0], s1r.at[k, 0], dev(nx if k == 0 else ny, c)) for k in range(2)]
    p1 = [[rdma(s1.at[k, pl.ds(256 * p, 256)], r1f.at[k - 2, c], s1s.at[k, p], s1r.at[k, c], dev(nx if k in (2, 4) else ny, p))
           for p in range(2)] for k in range(2, 6)]
    p1_in = [[rdma(s1.at[k, pl.ds(256 * p, 256)], r1f.at[k - 2, p], s1s.at[k, p], s1r.at[k, p], peer)
              for p in range(2)] for k in range(2, 6)]
    co = rdma(s1.at[pl.ds(6, 2), pl.ds(256 * (1 - c), 256)], o1r, os.at[0], orr.at[0], peer)
    cy = rdma(yp, yr, ys.at[0], yrs.at[0], peer)

    def copy_body(*refs):
        n = len(refs) // 2
        for i in range(n):
            refs[n + i][...] = refs[i][...]

    def a_phase():
        def body(x_ref, w_ref, a_ref, h_ref):
            j, k = pl.program_id(0), pl.program_id(1)

            @pl.when((k == 4) & (j < 3))
            def _():
                for d in w1_in(j + 1):
                    d.wait_recv()
                for d in w1_relay(j + 1):
                    d.start()

            @pl.when((k == 4) & (j < 2))
            def _():
                for d in w1_out(j + 2):
                    d.start()

            @pl.when((k == 4) & (j == 2))
            def _():
                for d in w2_out:
                    d.start()

            @pl.when((k == 6) & (j < 3))
            def _():
                for d in w1_relay_in(j + 1):
                    d.wait_recv()

            for n in range(B // SUB):
                s = slice(n * SUB, (n + 1) * SUB)
                a = jnp.dot(x_ref[s, :], w_ref[...], preferred_element_type=F32).astype(BF16)
                a_ref[s, :] = a
                h_ref[s, :] = _gelu(a.astype(F32)).astype(BF16)

        out = pl.BlockSpec((B, B), lambda j, k: (k, j))
        pltpu.emit_pipeline(body, grid=(4, T // B),
                            in_specs=[pl.BlockSpec((B, D), lambda j, k: (k, 0)), pl.BlockSpec((D, B), lambda j, k: (0, j))],
                            out_specs=[out, out])(xa, w1g, aa, ha)

    def e_phase(lo, n):
        def body(g_ref, w_ref, a_ref, d_ref):
            for m in range(B // SUB):
                s = slice(m * SUB, (m + 1) * SUB)
                e = lax.dot_general(g_ref[s, :], w_ref[...], (((1,), (1,)), ((), ())), preferred_element_type=F32)
                d_ref[s, :] = (_gelu_grad(a_ref[s, :].astype(F32)) * e).astype(BF16)

        act = pl.BlockSpec((B, B), lambda i, k: (k, blk(i + lo)))
        pltpu.emit_pipeline(body, grid=(n, T // B),
                            in_specs=[pl.BlockSpec((B, D), lambda i, k: (k, 0)),
                                      pl.BlockSpec((B, D), lambda i, k: (blk(i + lo), 0)), act],
                            out_specs=[act])(ga, w2g, aa, da)

    MS = 512

    def tn(parts, lhs, rhs, out, m, n, li, ri, out_spec, recv=(), at=None):
        def body(l_ref, r_ref, *rest):
            o_ref = rest[-1]
            if at is not None:
                @pl.when(pl.program_id(1) == 1)
                def _():
                    at(pl.program_id(0))

            @pl.when(pl.program_id(1) == 0)
            def _():
                o_ref[...] = jnp.zeros(o_ref.shape, F32)

            for r in rest[:-1]:
                @pl.when((pl.program_id(1) == 0) & (pl.program_id(0) < 2))
                def _():
                    o_ref[...] += r[...].reshape(o_ref.shape)

            for i in range(m // MS):
                s = slice(i * MS, (i + 1) * MS)
                o_ref[..., s, :] += lax.dot_general(l_ref[:, s], r_ref[...], (((0,), (0,)), ((), ())),
                                                    preferred_element_type=F32).reshape(o_ref.shape[:-2] + (MS, n))

        kt = 2048 if parts == 4 else B
        pltpu.emit_pipeline(body, grid=(parts, T // kt),
                            in_specs=[pl.BlockSpec((kt, m), lambda i, k: (k, li(i))), pl.BlockSpec((kt, n), lambda i, k: (k, ri(i)))]
                            + [pl.BlockSpec((1, m, n), functools.partial(lambda f, i, k: (f(i), 0, 0), f)) for _, f in recv],
                            out_specs=[out_spec])(lhs, rhs, *[r for r, _ in recv], out)

    half = pl.BlockSpec((1, B, B), lambda i, k: (i, 0, 0))
    half1 = pl.BlockSpec((1, 512, D), lambda i, k: (i, 0, 0))

    def first(i):
        return jnp.where(i < 2, nd, jnp.where(i == 2, nx, ny))

    def last(i):
        return jnp.where(i == 0, nx, jnp.where(i == 1, ny, q))

    other = lambda i: jnp.where(i == 0, 1, jnp.where(i == 1, 0, i - 2))

    def y_phase(own):
        def body(h_ref, w_ref, *rest):
            v = jnp.dot(h_ref[...], w_ref[...], preferred_element_type=F32)
            if own:
                x_ref, r_ref, o_ref = rest
                o_ref[...] = (x_ref[...].astype(F32) + (v + r_ref[...])).astype(BF16)
            else:
                rest[0][...] = v

        bm = 512
        base = 0 if own else TOK // bm
        col = pl.BlockSpec((bm, B), lambda n, i: (i, n))
        pltpu.emit_pipeline(body, grid=(2, (TOK // 2 if own else TOK) // bm),
                            in_specs=[pl.BlockSpec((bm, HF), lambda n, i: (i + base, 0)), pl.BlockSpec((HF, B), lambda n, i: (0, n))]
                            + ([col, col] if own else []),
                            out_specs=[col])(ha, w2g, *([x, yr] if own else []), y0 if own else yp)

    barrier = pltpu.get_barrier_semaphore()
    friends = [peer, dev(nx, 0), dev(nx, 1), dev(ny, 0), dev(ny, 1)]
    for d in friends:
        pl.semaphore_signal(barrier, inc=1, device_id=(d,), device_id_type=MESH)
    pl.semaphore_wait(barrier, len(friends))

    for d in w1_out(0):
        d.start()
    cx.start()
    cg.start()
    row = pl.BlockSpec((B, D), lambda i: (i, 0))
    pltpu.emit_pipeline(copy_body, grid=(4,),
                        in_specs=[pl.BlockSpec((256, B), lambda i: (0, 2 * i + c)), row],
                        out_specs=[pl.BlockSpec((256, B), lambda i: (me, i)), row])(w1, x, w1g, xa.at[pl.ds(0, TOK)])
    for d in w1_in(0):
        d.wait_recv()
    for d in w1_relay(0):
        d.start()
    for d in w1_out(1):
        d.start()
    pltpu.emit_pipeline(copy_body, grid=(4,),
                        in_specs=[pl.BlockSpec((256, D), lambda i: (i, 0)), row],
                        out_specs=[pl.BlockSpec((256, D), lambda i: (4 * q + i, 0)), row])(w2, g, w2g, ga.at[pl.ds(0, TOK)])
    cx.wait_recv()
    for d in w1_relay_in(0):
        d.wait_recv()
    with jax.named_scope("pa"):
        a_phase()
    cg.wait_recv()

    def at2(i):
        @pl.when(i == 1)
        def _():
            p2[0].start()

        @pl.when(i == 2)
        def _():
            p2[1].start()
            for d in w2_in:
                d.wait_recv()
            for d in w2_relay:
                d.start()

        @pl.when(i == 3)
        def _():
            p2[2].start()

    with jax.named_scope("d2diag"):
        tn(4, ha, ga, s2.at[pl.ds(0, 4)], B, B, first, lambda i: i % 2, half, at=at2)
    p2[3].start()
    with jax.named_scope("e3"):
        e_phase(0, 3)
    p2[0].wait_recv()
    p2[1].wait_recv()
    with jax.named_scope("d2add"):
        tn(2, ha, ga, s2.at[pl.ds(4, 2)], B, B, last, other, half, [(r2, lambda i: 1 - i)])
    p2[4].start()
    p2[5].start()
    for d in w2_relay_in:
        d.wait_recv()
    with jax.named_scope("e1"):
        e_phase(3, 1)

    def at1(i):
        @pl.when(i == 1)
        def _():
            p1d[0].start()

        @pl.when(i == 2)
        def _():
            p1d[1].start()

        @pl.when(i == 3)
        def _():
            for d in p1[0]:
                d.start()

    with jax.named_scope("d1diag"):
        tn(4, xa, da, s1.at[pl.ds(0, 4)], 512, D, first, lambda i: i % 2, half1, at=at1)
    for d in p1[1]:
        d.start()
    with jax.named_scope("ypeer"):
        y_phase(False)
    cy.start()
    p1d[0].wait_recv()
    p1d[1].wait_recv()

    def at1s(i):
        for k in (2, 3):
            @pl.when(i == k - 1)
            def _():
                for d in p1[k]:
                    d.start()

    with jax.named_scope("d1add"):
        tn(4, xa, da, s1.at[pl.ds(4, 4)], 512, D, last, other, half1, [(r1, lambda i: jnp.where(i == 0, 1, 0))], at=at1s)
    co.start()
    for k in range(2, 6):
        p2[k].wait_recv()
    with jax.named_scope("d2own"):
        tn(2, ha, ga, dw2, B, B, lambda i: q, lambda i: i, pl.BlockSpec((B, B), lambda i, k: (0, i)),
           [(r2, lambda i: 2 + i), (r2, lambda i: 5 - i)])
    cy.wait_recv()
    with jax.named_scope("yown"):
        y_phase(True)
    co.wait_recv()
    for pair in p1_in:
        for d in pair:
            d.wait_recv()
    for d in [cx, cg, co, cy] + w2_out + w2_relay + p2 + p1d + [d for pair in p1 for d in pair]:
        d.wait_send()

    @pl.loop(0, 4)
    def _(j):
        for d in w1_out(j) + w1_relay(j):
            d.wait_send()


def _finish(c_ref, h, w2, x, yr, y0, dw2, o1, o1r, fa, fb, y_out, dw1_out, dw2_out):
    for n in range(2):
        s = slice(n * B, (n + 1) * B)
        v = jnp.dot(h[...], w2[:, s], preferred_element_type=F32)
        y_out[1, :, s] = (x[:, s].astype(F32) + (v + yr[:, s])).astype(BF16)
    y_out[0] = y0[...]
    dw2_out[...] = dw2[...]
    own = jnp.where(pl.program_id(0) < 4, o1[0], o1r[0])
    dw1_out[...] = own + (fa[0, 0] + fb[0, 0])


def solution(mesh):
    spec = P(None, AX, None)

    def body(x, g, w1, w2):
        c = lax.axis_index(AX) % 2
        shape = lambda s, t: jax.ShapeDtypeStruct(s, t)
        dma = lambda *s: pltpu.SemaphoreType.DMA(s)
        hbm = pl.BlockSpec(memory_space=pl.ANY)
        x = x.reshape(TOK, D)
        outs = [
            shape((T, HF), BF16), shape((HF, D), BF16), shape((TOK, D), F32), shape((TOK // 2, D), BF16), shape((B, D), F32),
            shape((8, 512, D), F32), shape((2, 256, D), F32), shape((4, 2, 256, D), F32),
            shape((T, D), BF16), shape((T, D), BF16), shape((D, HF), BF16), shape((T, HF), BF16), shape((T, HF), BF16),
            shape((6, B, B), F32), shape((6, B, B), F32), shape((2, 512, D), F32), shape((TOK, D), F32),
        ]
        res = pl.pallas_call(
            _kernel,
            out_shape=outs,
            in_specs=[hbm] * 4,
            out_specs=[hbm] * len(outs),
            scratch_shapes=[dma(2), dma(2), dma(4, 7), dma(4, 7), dma(4), dma(4), dma(6), dma(6), dma(6, 2), dma(6, 2),
                            dma(1), dma(1), dma(1), dma(1)],
            compiler_params=pltpu.CompilerParams(collective_id=0, has_side_effects=True, vmem_limit_bytes=VMEM),
            name="step",
        )(x, g.reshape(TOK, D), w1[0], w2[0])
        h, w2g, yr, y0, dw2, s1, o1r, r1f = res[:8]
        part = lambda s, c: (s // 4) * (1 - c[0]) + (1 - s // 4) * c[0]
        n, t = (lambda s: (s // 2) % 2), (lambda s: s % 2)
        mine = lambda s: jnp.minimum(s, 3)
        theirs = lambda s: jnp.maximum(s, 4)
        bm = TOK // 16
        row = lambda m, w=D, lo=0: pl.BlockSpec((m, w), lambda s, c: (s + lo, 0))
        y, dw1, dw2 = pl.pallas_call(
            _finish,
            grid_spec=pltpu.PrefetchScalarGridSpec(
                num_scalar_prefetch=1,
                grid=(8,),
                in_specs=[
                    row(bm, HF, 8), pl.BlockSpec((HF, D), lambda s, c: (0, 0), pipeline_mode=pl.Buffered(1)), row(bm, D, 8), row(bm, D, 8),
                    row(bm), row(B // 8),
                    pl.BlockSpec((1, 256, B), lambda s, c: (6 + n(mine(s)), c[0], t(mine(s)))),
                    pl.BlockSpec((1, 256, B), lambda s, c: (n(theirs(s)), 0, t(theirs(s)))),
                    pl.BlockSpec((1, 1, 256, B), lambda s, c: (n(s), part(s, c), 0, t(s))),
                    pl.BlockSpec((1, 1, 256, B), lambda s, c: (3 - n(s), part(s, c), 0, t(s))),
                ],
                out_specs=[pl.BlockSpec((2, bm, D), lambda s, c: (0, s, 0)), pl.BlockSpec((256, B), lambda s, c: (0, 2 * (2 * n(s) + t(s)) + part(s, c))), row(B // 8)],
            ),
            out_shape=[shape((2, TOK // 2, D), BF16), shape((256, 8192), F32), shape((B, D), F32)],
            compiler_params=pltpu.CompilerParams(dimension_semantics=("arbitrary",), vmem_limit_bytes=VMEM),
            name="finish",
        )(c[None], h, w2g, x, yr, y0, dw2, s1, o1r, r1f, r1f)
        return y, dw1[None], dw2[None]

    return jax.shard_map(body, mesh=mesh, in_specs=(spec, spec, spec, spec),
                         out_specs=(spec, spec, spec), check_vma=False)
```

time: 991 us -> 940 us (0.949)
  Pallas kernels: 990 us -> 931 us
    pallas_call x1, Pallas kernels: 960 us -> 876 us  [body(): pl.pallas_call(_kernel, out_shape=outs, in_specs=[hbm] * 4, out_specs=[hb...]
    pallas_call x1, Pallas kernels: 30.1 us -> 54.4 us  [body(): pl.pallas_call(_finish, grid_spec=pltpu.PrefetchScalarGridSpec(num_scalar...]
where the time goes in v3:
time: 940 us; the launch traced here: 932 us
  Pallas kernels  931 us (99%)
    pallas_call x1, Pallas kernels, body(): pl.pallas_call(_kernel, out_shape=outs, in_specs=[hbm] * 4, out_specs=[hb...  876 us
    pallas_call x1, Pallas kernels, body(): pl.pallas_call(_finish, grid_spec=pltpu.PrefetchScalarGridSpec(num_scalar...  54.4 us

profile of v3, /device:TPU:1, one launch (start us, length us, event | category | flops | bytes accessed | tf_op | source)
XLA Modules:
  0.0 931.8 jit_solution(432414894673533465)
XLA Ops:
  0.6 876.3 %step.1 = (bf16[8192,4096]{1,0:T(8,128)(2,1)}, bf16[4096,2048]{1,0:T(8,128)(2,1)}, f32[4096,2048]{1,0:T(8,128)}, bf16[2048,2048]{1,0:T(8,128)(2,1)}, f32[1024,20...) custom-call(bf16[4096,2048]{1,0:T(8,128)(2,1)} %bitcast.7, ...), custom_call_target="tpu_custom_call" | custom-call | tf_op jit(solution)/shard_map/step/pallas_call | solution.py:359
  877.0 54.4 %finish.1 = (bf16[2,2048,2048]{2,1,0:T(8,128)(2,1)}, f32[256,8192]{1,0:T(8,128)}, f32[1024,2048]{1,0:T(8,128)}) custom-call(s32[1]{0:T(128)} %bitcast.c_ref, bf16[8192,4096]{1,0:T(8,128)(2,1)} %get-tuple-element.14.h, bf16[4096,2048]{1,0:T(8,128)(2,1)} %get-tuple-element.15.w2, bf16[4096,2048]{1,0:T(8,128)(2,1)} %bitcast.8, ...), custom_call_target="tpu_custom_call" | custom-call | tf_op jit(solution)/shard_map/finish/pallas_call | solution.py:376

commit v4 on v3

--- a/solution.py
+++ b/solution.py
@@ -178,7 +178,7 @@
                 o_ref[..., s, :] += lax.dot_general(l_ref[:, s], r_ref[...], (((0,), (0,)), ((), ())),
                                                     preferred_element_type=F32).reshape(o_ref.shape[:-2] + (MS, n))
 
-        kt = 2048 if parts == 4 else B
+        kt = B
         pltpu.emit_pipeline(body, grid=(parts, T // kt),
                             in_specs=[pl.BlockSpec((kt, m), lambda i, k: (k, li(i))), pl.BlockSpec((kt, n), lambda i, k: (k, ri(i)))]
                             + [pl.BlockSpec((1, m, n), functools.partial(lambda f, i, k: (f(i), 0, 0), f)) for _, f in recv],
@@ -207,7 +207,7 @@
         bm = 512
         base = 0 if own else TOK // bm
         col = pl.BlockSpec((bm, B), lambda n, i: (i, n))
-        pltpu.emit_pipeline(body, grid=(2, (TOK // 2 if own else TOK) // bm),
+        pltpu.emit_pipeline(body, grid=(2, (TOK // 4 if own else TOK) // bm),
                             in_specs=[pl.BlockSpec((bm, HF), lambda n, i: (i + base, 0)), pl.BlockSpec((HF, B), lambda n, i: (0, n))]
                             + ([col, col] if own else []),
                             out_specs=[col])(ha, w2g, *([x, yr] if own else []), y0 if own else yp)
@@ -330,11 +330,14 @@
             d.wait_send()
 
 
-def _finish(c_ref, h, w2, x, yr, y0, dw2, o1, o1r, fa, fb, y_out, dw1_out, dw2_out):
+def _finish(c_ref, ha, hb, hc, w2, xa, xb, xc, ra, rb, rc, y0, dw2, o1, o1r, fa, fb, y_out, dw1_out, dw2_out):
+    h = jnp.concatenate([ha[0], hb[0], hc[0]], axis=0)
+    m = ha.shape[1]
     for n in range(2):
         s = slice(n * B, (n + 1) * B)
-        v = jnp.dot(h[...], w2[:, s], preferred_element_type=F32)
-        y_out[1, :, s] = (x[:, s].astype(F32) + (v + yr[:, s])).astype(BF16)
+        v = jnp.dot(h, w2[:, s], preferred_element_type=F32)
+        for i, (x, r) in enumerate(((xa, ra), (xb, rb), (xc, rc))):
+            y_out[i + 1, :, s] = (x[0, :, s].astype(F32) + (v[i * m:(i + 1) * m] + r[0, :, s])).astype(BF16)
     y_out[0] = y0[...]
     dw2_out[...] = dw2[...]
     own = jnp.where(pl.program_id(0) < 4, o1[0], o1r[0])
@@ -351,7 +354,7 @@
         hbm = pl.BlockSpec(memory_space=pl.ANY)
         x = x.reshape(TOK, D)
         outs = [
-            shape((T, HF), BF16), shape((HF, D), BF16), shape((TOK, D), F32), shape((TOK // 2, D), BF16), shape((B, D), F32),
+            shape((T, HF), BF16), shape((HF, D), BF16), shape((TOK, D), F32), shape((TOK // 4, D), BF16), shape((B, D), F32),
             shape((8, 512, D), F32), shape((2, 256, D), F32), shape((4, 2, 256, D), F32),
             shape((T, D), BF16), shape((T, D), BF16), shape((D, HF), BF16), shape((T, HF), BF16), shape((T, HF), BF16),
             shape((6, B, B), F32), shape((6, B, B), F32), shape((2, 512, D), F32), shape((TOK, D), F32),
@@ -371,28 +374,30 @@
         n, t = (lambda s: (s // 2) % 2), (lambda s: s % 2)
         mine = lambda s: jnp.minimum(s, 3)
         theirs = lambda s: jnp.maximum(s, 4)
-        bm = TOK // 16
-        row = lambda m, w=D, lo=0: pl.BlockSpec((m, w), lambda s, c: (s + lo, 0))
+        bm = TOK // 32
+        row = lambda m, w=D: pl.BlockSpec((m, w), lambda s, c: (s, 0))
+        quarters = lambda w: [pl.BlockSpec((1, bm, w), functools.partial(lambda i, s, c: (i, s, 0), i)) for i in (1, 2, 3)]
+        h, x, yr = h.reshape(8, TOK // 4, HF), x.reshape(4, TOK // 4, D), yr.reshape(4, TOK // 4, D)
         y, dw1, dw2 = pl.pallas_call(
             _finish,
             grid_spec=pltpu.PrefetchScalarGridSpec(
                 num_scalar_prefetch=1,
                 grid=(8,),
-                in_specs=[
-                    row(bm, HF, 8), pl.BlockSpec((HF, D), lambda s, c: (0, 0), pipeline_mode=pl.Buffered(1)), row(bm, D, 8), row(bm, D, 8),
+                in_specs=quarters(HF) + [pl.BlockSpec((HF, D), lambda s, c: (0, 0), pipeline_mode=pl.Buffered(1))]
+                + quarters(D) + quarters(D) + [
                     row(bm), row(B // 8),
                     pl.BlockSpec((1, 256, B), lambda s, c: (6 + n(mine(s)), c[0], t(mine(s)))),
                     pl.BlockSpec((1, 256, B), lambda s, c: (n(theirs(s)), 0, t(theirs(s)))),
                     pl.BlockSpec((1, 1, 256, B), lambda s, c: (n(s), part(s, c), 0, t(s))),
                     pl.BlockSpec((1, 1, 256, B), lambda s, c: (3 - n(s), part(s, c), 0, t(s))),
                 ],
-                out_specs=[pl.BlockSpec((2, bm, D), lambda s, c: (0, s, 0)), pl.BlockSpec((256, B), lambda s, c: (0, 2 * (2 * n(s) + t(s)) + part(s, c))), row(B // 8)],
+                out_specs=[pl.BlockSpec((4, bm, D), lambda s, c: (0, s, 0)), pl.BlockSpec((256, B), lambda s, c: (0, 2 * (2 * n(s) + t(s)) + part(s, c))), row(B // 8)],
             ),
-            out_shape=[shape((2, TOK // 2, D), BF16), shape((256, 8192), F32), shape((B, D), F32)],
+            out_shape=[shape((4, TOK // 4, D), BF16), shape((256, 8192), F32), shape((B, D), F32)],
             compiler_params=pltpu.CompilerParams(dimension_semantics=("arbitrary",), vmem_limit_bytes=VMEM),
             name="finish",
-        )(c[None], h, w2g, x, yr, y0, dw2, s1, o1r, r1f, r1f)
-        return y, dw1[None], dw2[None]
+        )(c[None], h, h, h, w2g, x, x, x, yr, yr, yr, y0, dw2, s1, o1r, r1f, r1f)
+        return y.reshape(2, TOK // 2, D), dw1[None], dw2[None]
 
     return jax.shard_map(body, mesh=mesh, in_specs=(spec, spec, spec, spec),
                          out_specs=(spec, spec, spec), check_vma=False)

time: 940 us -> 949 us (level)
  Pallas kernels: 931 us -> 947 us
    pallas_call x1, Pallas kernels: 54.4 us -> 70.6 us  [body(): pl.pallas_call(_finish, grid_spec=pltpu.PrefetchScalarGridSpec(num_scalar...]
where the time goes in v4:
time: 949 us; the launch traced here: 948 us
  Pallas kernels  947 us (100%)
    pallas_call x1, Pallas kernels, body(): pl.pallas_call(_kernel, out_shape=outs, in_specs=[hbm] * 4, out_specs=[hb...  877 us
    pallas_call x1, Pallas kernels, body(): pl.pallas_call(_finish, grid_spec=pltpu.PrefetchScalarGridSpec(num_scalar...  70.6 us

profile of v4, /device:TPU:1, one launch (start us, length us, event | category | flops | bytes accessed | tf_op | source)
XLA Modules:
  0.0 948.3 jit_solution(10664350342763969558)
XLA Ops:
  0.6 876.9 %step.1 = (bf16[8192,4096]{1,0:T(8,128)(2,1)}, bf16[4096,2048]{1,0:T(8,128)(2,1)}, f32[4096,2048]{1,0:T(8,128)}, bf16[1024,2048]{1,0:T(8,128)(2,1)}, f32[1024,20...) custom-call(bf16[4096,2048]{1,0:T(8,128)(2,1)} %bitcast.14, ...), custom_call_target="tpu_custom_call" | custom-call | tf_op jit(solution)/shard_map/step/pallas_call | solution.py:362
  877.6 70.6 %finish.1 = (bf16[4,1024,2048]{2,1,0:T(8,128)(2,1)}, f32[256,8192]{1,0:T(8,128)}, f32[1024,2048]{1,0:T(8,128)}) custom-call(s32[1]{0:T(128)} %bitcast.c_ref, bf16[8,1024,4096]{2,1,0:T(8,128)(2,1)} %bitcast.5.ha.hb.hc, bf16[8,1024,4096]{2,1,0:T(8,128)(2,1)} %bitcast.5.ha.hb.hc, bf16[8,1024,4096]{2,1,0:T(8,128)(2,1)} %bitcast.5.ha.hb.hc, ...), custom_call_target="tpu_custom_call" | custom-call | tf_op jit(solution)/shard_map/finish/pallas_call | solution.py:381
